TPU v7x, 32 devices: a whole 2x2x4 slice. The times are simulated.
32 devices in a mesh: dp: 16 (over z, y, core), fsdp: 2 (over x).
Axes of the slice: x: 2, y: 2, z: 4, core: 2. Of those that a mesh axis runs over, the one named last changes fastest.
Arguments:
- patches: bfloat16 [16384, 768], P(('dp', 'fsdp')), may hold values from -6 to 6
- cotangent: bfloat16 [16384, 768], P(('dp', 'fsdp')), may hold values from -6 to 6
- lengths: int32 [32, 4], P(('dp', 'fsdp')), may hold values from 0 to 512, as said below
- arrange: int32 [16384], P(('dp', 'fsdp')), may hold values from 0 to 511, as said below
- first_gain: bfloat16 [768], P('dp'), may hold values from 0.3984375 to 1.59375
- first_shift: bfloat16 [768], P('dp'), may hold values from -1.5 to 1.5
- project_weight: bfloat16 [768, 2304], P('dp', 'fsdp'), may hold values from -0.21875 to 0.21875
- query_bias: bfloat16 [768], P('dp'), may hold values from -1.5 to 1.5
- value_bias: bfloat16 [768], P('dp'), may hold values from -1.5 to 1.5
- output_weight: bfloat16 [768, 768], P('dp', 'fsdp'), may hold values from -1.75 to 1.75
- output_bias: bfloat16 [768], P('dp'), may hold values from -1.5 to 1.5
- second_gain: bfloat16 [768], P('dp'), may hold values from 0.3984375 to 1.59375
- second_shift: bfloat16 [768], P('dp'), may hold values from -1.5 to 1.5
- up_weight: bfloat16 [768, 3072], P('dp', 'fsdp'), may hold values from -0.21875 to 0.21875
- up_bias: bfloat16 [3072], P('dp'), may hold values from -1.5 to 1.5
- down_weight: bfloat16 [3072, 768], P('dp', 'fsdp'), may hold values from -0.109375 to 0.109375
- down_bias: bfloat16 [768], P('dp'), may hold values from -1.5 to 1.5
Outputs:
- encoded: bfloat16 [16384, 768], P(('dp', 'fsdp'))
- grad_patches: bfloat16 [16384, 768], P(('dp', 'fsdp'))
- grad_first_gain: float32 [768], P('dp')
- grad_first_shift: float32 [768], P('dp')
- grad_project_weight: float32 [768, 2304], P('dp', 'fsdp')
- grad_query_bias: float32 [768], P('dp')
- grad_value_bias: float32 [768], P('dp')
- grad_output_weight: float32 [768, 768], P('dp', 'fsdp')
- grad_output_bias: float32 [768], P('dp')
- grad_second_gain: float32 [768], P('dp')
- grad_second_shift: float32 [768], P('dp')
- grad_up_weight: float32 [768, 3072], P('dp', 'fsdp')
- grad_up_bias: float32 [3072], P('dp')
- grad_down_weight: float32 [3072, 768], P('dp', 'fsdp')
- grad_down_bias: float32 [768], P('dp')
Inputs may be any that keep to these rules, and one draw needn't show every extreme that they name: Each block's 4 lengths sum to at least 384 and at most 512; slots may be empty; in every draw some block holds a single sequence of 512 rows. `arrange`: each block's 512 entries are a permutation of 0 to 511.
All inputs are finite; a program needn't handle non-finite values.
Results may differ from a plain program's by a relative error of at most 0.012.
Values may be sent and summed in bfloat16 or wider, within the bound.
A program may use at most 128 MiB of HBM per device.

v0:
```python
import jax
import jax.numpy as jnp
from jax import lax
from jax.sharding import PartitionSpec as P

HEADS = 12
HEAD = 64
NORM_EPSILON = 1e-12
MASK_VALUE = -1e30
ROOT_HALF = 0.7071067811865476


def norm_rows(values, norm_gain, norm_shift):
    center = values - jnp.mean(values, axis=-1, keepdims=True)
    spread = jnp.mean(center * center, axis=-1, keepdims=True)
    return center * lax.rsqrt(spread + NORM_EPSILON) * norm_gain + norm_shift


def gelu_exact(values):
    return 0.5 * values * (1.0 + lax.erf(values * ROOT_HALF))


def slot_labels(lengths, arrange):
    total_rows = arrange.shape[0]
    slot_ends = jnp.cumsum(lengths[0])
    position = jnp.arange(total_rows, dtype=jnp.int32)
    slot_index = jnp.sum((position[:, None] >= slot_ends[None, :]).astype(jnp.int32), axis=1)
    return jnp.zeros((total_rows,), jnp.int32).at[arrange].set(slot_index)


def matmul(left_side, right_side, pattern):
    return jnp.einsum(pattern, left_side, right_side, preferred_element_type=jnp.float32)


def column_sums(values):
    return jnp.sum(values.astype(jnp.float32), axis=0)


def local(
    patches,
    cotangent,
    lengths,
    arrange,
    first_gain,
    first_shift,
    project_weight,
    query_bias,
    value_bias,
    output_weight,
    output_bias,
    second_gain,
    second_shift,
    up_weight,
    up_bias,
    down_weight,
    down_bias,
):
    arrived, cot_rows = (
        lax.all_to_all(patches, "dp", split_axis=0, concat_axis=0, tiled=True),
        lax.all_to_all(cotangent, "dp", split_axis=0, concat_axis=0, tiled=True),
    )
    total_rows, width = patches.shape
    labels = slot_labels(lengths, arrange)
    live_rows = (labels < lengths.shape[1]).astype(jnp.float32)[:, None]
    project_part, output_part, up_part, down_part = (
        lax.all_gather(project_weight, "fsdp", axis=1, tiled=True),
        lax.all_gather(output_weight, "fsdp", axis=1, tiled=True),
        lax.all_gather(up_weight, "fsdp", axis=1, tiled=True),
        lax.all_gather(down_weight, "fsdp", axis=1, tiled=True),
    )
    attn_set = (
        lax.all_gather(first_gain, "dp", axis=0, tiled=True),
        lax.all_gather(first_shift, "dp", axis=0, tiled=True),
        lax.all_gather(project_part, "dp", axis=0, tiled=True),
        lax.all_gather(query_bias, "dp", axis=0, tiled=True),
        lax.all_gather(value_bias, "dp", axis=0, tiled=True),
        lax.all_gather(output_part, "dp", axis=0, tiled=True),
        lax.all_gather(output_bias, "dp", axis=0, tiled=True),
    )
    inputs = arrived.astype(jnp.float32)
    gain_one = attn_set[0].astype(jnp.float32)
    shift_one = attn_set[1].astype(jnp.float32)
    normed_one = norm_rows(inputs, gain_one, shift_one)
    normed_low = normed_one.astype(jnp.bfloat16)
    joint = jnp.dot(normed_low, attn_set[2], preferred_element_type=jnp.float32)
    queries = (
        (joint[:, :width] + attn_set[3].astype(jnp.float32))
        .astype(jnp.bfloat16)
        .reshape(total_rows, HEADS, HEAD)
    )
    key_rows = joint[:, width : 2 * width].astype(jnp.bfloat16).reshape(total_rows, HEADS, HEAD)
    value_rows = (
        (joint[:, 2 * width :] + attn_set[4].astype(jnp.float32))
        .astype(jnp.bfloat16)
        .reshape(total_rows, HEADS, HEAD)
    )
    score_scale = HEAD ** (-0.5)
    block_rows = min(512, total_rows)
    block_starts = jnp.arange(total_rows // block_rows, dtype=jnp.int32) * block_rows

    def block_scores():
        raw_scores = matmul(queries, key_rows, "qhe,khe->hqk") * score_scale
        visible = labels[:, None] == labels[None, :]
        return (queries, jnp.where(visible[None], raw_scores, MASK_VALUE))

    def attend(start):
        query_block, scores = block_scores()
        top_score = jnp.max(scores, axis=-1, keepdims=True)
        weights = jnp.exp(scores - top_score)
        totals = jnp.sum(weights, axis=-1, keepdims=True)
        prob_low = (weights / totals).astype(jnp.bfloat16)
        mixed_rows = matmul(prob_low, value_rows, "hqk,khe->qhe")
        return (mixed_rows.astype(jnp.bfloat16), (top_score + jnp.log(totals))[:, :, 0])

    mixed_blocks, log_totals = lax.map(attend, block_starts)
    attended = mixed_blocks.reshape(total_rows, width)
    attn_out = jnp.dot(attended, attn_set[5], preferred_element_type=jnp.float32) + attn_set[
        6
    ].astype(jnp.float32)
    hidden = inputs + attn_out
    mlp_set = (
        lax.all_gather(second_gain, "dp", axis=0, tiled=True),
        lax.all_gather(second_shift, "dp", axis=0, tiled=True),
        lax.all_gather(up_part, "dp", axis=0, tiled=True),
        lax.all_gather(up_bias, "dp", axis=0, tiled=True),
        lax.all_gather(down_part, "dp", axis=0, tiled=True),
        lax.all_gather(down_bias, "dp", axis=0, tiled=True),
    )
    gain_two = mlp_set[0].astype(jnp.float32)
    shift_two = mlp_set[1].astype(jnp.float32)
    normed_two = norm_rows(hidden, gain_two, shift_two)
    normed_two_low = normed_two.astype(jnp.bfloat16)
    pre_act = jnp.dot(normed_two_low, mlp_set[2], preferred_element_type=jnp.float32) + mlp_set[
        3
    ].astype(jnp.float32)
    activated = gelu_exact(pre_act).astype(jnp.bfloat16)
    branch = jnp.dot(activated, mlp_set[4], preferred_element_type=jnp.float32) + mlp_set[5].astype(
        jnp.float32
    )
    encoded_rows = live_rows * (hidden + branch)
    grad_out = live_rows * cot_rows.astype(jnp.float32)
    grad_branch = grad_out.astype(jnp.bfloat16)
    again_two = (
        lax.all_gather(second_gain, "dp", axis=0, tiled=True),
        lax.all_gather(second_shift, "dp", axis=0, tiled=True),
        lax.all_gather(up_part, "dp", axis=0, tiled=True),
        lax.all_gather(up_bias, "dp", axis=0, tiled=True),
        lax.all_gather(down_part, "dp", axis=0, tiled=True),
        lax.all_gather(down_bias, "dp", axis=0, tiled=True),
    )
    grad_down = matmul(activated, grad_branch, "tf,td->fd")
    grad_downbias = column_sums(grad_branch)
    grad_activ = matmul(grad_branch, again_two[4], "td,fd->tf")
    grad_pre = jax.vjp(gelu_exact, pre_act)[1](grad_activ)[0].astype(jnp.bfloat16)
    grad_up = matmul(normed_two_low, grad_pre, "td,tf->df")
    grad_upbias = column_sums(grad_pre)
    grad_normed_two = matmul(grad_pre, again_two[2], "tf,df->td")
    norm_pull_two = jax.vjp(
        norm_rows, hidden, again_two[0].astype(jnp.float32), again_two[1].astype(jnp.float32)
    )[1]
    grad_hidden_part, grad_gain_two, grad_shift_two = norm_pull_two(grad_normed_two)
    grad_hidden = grad_out + grad_hidden_part
    mlp_sums = (
        lax.psum_scatter(grad_up, "dp", scatter_dimension=0, tiled=True),
        lax.psum_scatter(grad_down, "dp", scatter_dimension=0, tiled=True),
        lax.psum_scatter(grad_gain_two, "dp", scatter_dimension=0, tiled=True),
        lax.psum_scatter(grad_shift_two, "dp", scatter_dimension=0, tiled=True),
        lax.psum_scatter(grad_upbias, "dp", scatter_dimension=0, tiled=True),
        lax.psum_scatter(grad_downbias, "dp", scatter_dimension=0, tiled=True),
    )
    again_one = (
        lax.all_gather(first_gain, "dp", axis=0, tiled=True),
        lax.all_gather(first_shift, "dp", axis=0, tiled=True),
        lax.all_gather(project_part, "dp", axis=0, tiled=True),
        lax.all_gather(query_bias, "dp", axis=0, tiled=True),
        lax.all_gather(value_bias, "dp", axis=0, tiled=True),
        lax.all_gather(output_part, "dp", axis=0, tiled=True),
        lax.all_gather(output_bias, "dp", axis=0, tiled=True),
    )
    grad_attn = grad_hidden.astype(jnp.bfloat16)
    grad_output = matmul(attended, grad_attn, "td,te->de")
    grad_outbias = column_sums(grad_attn)
    grad_attended = (
        matmul(grad_attn, again_one[5], "te,de->td")
        .astype(jnp.bfloat16)
        .reshape(total_rows, HEADS, HEAD)
    )

    def back_block(carry, block_item):
        key_acc, value_acc = carry
        start, log_block = block_item
        query_block, scores = block_scores()
        prob_full = jnp.exp(scores - log_block[:, :, None])
        prob_low = prob_full.astype(jnp.bfloat16)
        value_acc = value_acc + matmul(prob_low, grad_attended, "hqk,qhe->khe")
        grad_prob = matmul(grad_attended, value_rows, "qhe,khe->hqk")
        inner = jnp.sum(prob_full * grad_prob, axis=-1, keepdims=True)
        grad_scores = (prob_full * (grad_prob - inner)).astype(jnp.bfloat16)
        query_grad = matmul(grad_scores, key_rows, "hqk,khe->qhe") * score_scale
        key_acc = key_acc + matmul(grad_scores, query_block, "hqk,qhe->khe") * score_scale
        return ((key_acc, value_acc), query_grad.astype(jnp.bfloat16))

    zero_acc = jnp.zeros((total_rows, HEADS, HEAD), jnp.float32)
    (key_grad_sum, value_grad_sum), query_grads = lax.scan(
        back_block, (zero_acc, zero_acc), (block_starts, log_totals)
    )
    grad_queries = query_grads.reshape(total_rows, width)
    grad_keys = key_grad_sum.reshape(total_rows, width).astype(jnp.bfloat16)
    grad_values = value_grad_sum.reshape(total_rows, width).astype(jnp.bfloat16)
    grad_joint = jnp.concatenate([grad_queries, grad_keys, grad_values], axis=1)
    grad_project = matmul(normed_low, grad_joint, "td,tf->df")
    grad_querybias = column_sums(grad_queries)
    grad_valuebias = column_sums(grad_values)
    grad_normed_one = matmul(grad_joint, again_one[2], "tf,df->td")
    norm_pull_one = jax.vjp(
        norm_rows, inputs, again_one[0].astype(jnp.float32), again_one[1].astype(jnp.float32)
    )[1]
    grad_input_part, grad_gain_one, grad_shift_one = norm_pull_one(grad_normed_one)
    grad_inputs = grad_hidden + grad_input_part
    attn_sums = (
        lax.psum_scatter(grad_project, "dp", scatter_dimension=0, tiled=True),
        lax.psum_scatter(grad_output, "dp", scatter_dimension=0, tiled=True),
        lax.psum_scatter(grad_gain_one, "dp", scatter_dimension=0, tiled=True),
        lax.psum_scatter(grad_shift_one, "dp", scatter_dimension=0, tiled=True),
        lax.psum_scatter(grad_querybias, "dp", scatter_dimension=0, tiled=True),
        lax.psum_scatter(grad_valuebias, "dp", scatter_dimension=0, tiled=True),
        lax.psum_scatter(grad_outbias, "dp", scatter_dimension=0, tiled=True),
    )
    matrix_parts = (
        lax.psum_scatter(
            attn_sums[0].astype(jnp.bfloat16), "fsdp", scatter_dimension=1, tiled=True
        ).astype(jnp.float32),
        lax.psum_scatter(
            attn_sums[1].astype(jnp.bfloat16), "fsdp", scatter_dimension=1, tiled=True
        ).astype(jnp.float32),
        lax.psum_scatter(
            mlp_sums[0].astype(jnp.bfloat16), "fsdp", scatter_dimension=1, tiled=True
        ).astype(jnp.float32),
        lax.psum_scatter(
            mlp_sums[1].astype(jnp.bfloat16), "fsdp", scatter_dimension=1, tiled=True
        ).astype(jnp.float32),
    )
    vector_parts = lax.psum(
        (
            attn_sums[2],
            attn_sums[3],
            attn_sums[4],
            attn_sums[5],
            attn_sums[6],
            mlp_sums[2],
            mlp_sums[3],
            mlp_sums[4],
            mlp_sums[5],
        ),
        "fsdp",
    )
    encoded_back, grad_back = (
        lax.all_to_all(
            encoded_rows.astype(jnp.bfloat16), "dp", split_axis=0, concat_axis=0, tiled=True
        ),
        lax.all_to_all(
            grad_inputs.astype(jnp.bfloat16), "dp", split_axis=0, concat_axis=0, tiled=True
        ),
    )
    return (
        encoded_back,
        grad_back,
        vector_parts[0],
        vector_parts[1],
        matrix_parts[0],
        vector_parts[2],
        vector_parts[3],
        matrix_parts[1],
        vector_parts[4],
        vector_parts[5],
        vector_parts[6],
        matrix_parts[2],
        vector_parts[7],
        matrix_parts[3],
        vector_parts[8],
    )


def solution(mesh):
    return jax.shard_map(
        local,
        mesh=mesh,
        in_specs=(
            P(("dp", "fsdp"), None),
            P(("dp", "fsdp"), None),
            P(("dp", "fsdp"), None),
            P(("dp", "fsdp")),
            P("dp"),
            P("dp"),
            P("dp", "fsdp"),
            P("dp"),
            P("dp"),
            P("dp", "fsdp"),
            P("dp"),
            P("dp"),
            P("dp"),
            P("dp", "fsdp"),
            P("dp"),
            P("dp", "fsdp"),
            P("dp"),
        ),
        out_specs=(
            P(("dp", "fsdp"), None),
            P(("dp", "fsdp"), None),
            P("dp"),
            P("dp"),
            P("dp", "fsdp"),
            P("dp"),
            P("dp"),
            P("dp", "fsdp"),
            P("dp"),
            P("dp"),
            P("dp"),
            P("dp", "fsdp"),
            P("dp"),
            P("dp", "fsdp"),
            P("dp"),
        ),
        check_vma=False,
    )
```

profile of v0, /device:TPU:0, one launch (start us, length us, event | category | flops | bytes accessed | tf_op | source)
XLA Modules:
  0.0 716.2 jit_solution(9440607187867650082)
XLA Ops:
  7.2 8.7 %all_gather.59 = bf16[48,2304]{1,0:T(8,128)(2,1)} all-gather(bf16[48,1152]{1,0:T(8,128)(2,1)} %param.23), channel_id=1, replica_groups=mesh['dp'=16,'fsdp'=2] {'fsdp'}, dimensions={1}, use_global_device_ids=true | all-gather | bytes 331776 | tf_op jit(solution)/shard_map/all_gather | solution.py:66
  16.0 4.9 all_gather.63
  21.1 7.0 all_gather.68
  28.2 6.0 all-to-all-start
  34.2 6.9 all_gather.71
  41.4 14.7 %all-to-all-done = bf16[16,32,768]{2,1,0:T(8,128)(2,1)S(1)} async-done(((bf16[16,32,768]{2,1,0:T(8,128)(2,1)}), bf16[16,32,768]{2,1,0:T(8,128)(2,1)S(1)}, u32[]{:S(2)}, u32[]{:S(2)}) %all-to-all-start) | async-done | bytes 786464 | tf_op jit(solution)/shard_map/all_to_all | solution.py:59
  56.1 14.3 %all-to-all-start.2 = ((bf16[16,32,768]{2,1,0:T(8,128)(2,1)}), bf16[16,32,768]{2,1,0:T(8,128)(2,1)S(1)}, u32[]{:S(2)}, u32[]{:S(2)}) async-start(bf16[16,32,768]{2,1,0:T(8,128)(2,1)} %bitcast.13), calls=%async_computation.2 | async-start | bytes 1572864 | tf_op jit(solution)/shard_map/all_to_all | solution.py:60
  74.6 66.2 %all-reduce.20 = (bf16[768]{0:T(1024)(128)(2,1)S(1)}, bf16[768]{0:T(1024)(128)(2,1)S(1)}, bf16[768]{0:T(1024)(128)(2,1)S(1)}, bf16[768]{0:T(1024)(128)(2,1)S(1)}...) all-reduce(bf16[768]{0:T(1024)(128)(2,1)S(1)} %dynamic-update-slice, ...), channel_id=1, replica_groups=mesh['dp'=16,'fsdp'=2] {'dp'}, use_global_device_ids=true, to_apply=%add.1 | all-reduce | flops 9216 | bytes 36864
  141.4 2.9 scatter_custom_fusion
  146.7 4.3 fusion.45
  152.0 1.2 fusion.7
  153.5 1.7 copy.62
  155.2 2.6 copy.60
  157.8 2.1 fusion.6
  159.9 2.6 fusion
  162.4 2.0 copy-done
  164.5 4.5 fusion.24
  169.0 2.5 fusion.44
  171.8 7.2 %fusion.39 = f32[512,3072]{1,0:T(8,128)} fusion(bf16[768,3072]{1,0:T(8,128)(2,1)} %all-gather.9.cloned.1.call-done, f32[512,768]{1,0:T(8,128)S(1)} %get-tuple-element.114, f32[768]{0:T(1024)} %convert_element_type.197, f32[768]{0:T(1024)S(1)} %convert_element_type.196, f32[512]{0:T(512)S(1)} %fusion.28, f32[512]{0:T(512)S(1)} %broadcast_multiply_fusion.1), kind=kOutput, calls=%fused_computation.87 | convolution fusion | flops 2417885184 | bytes 12593152 | tf_op jit(solution)/shard_map/dot_general | solution.py:133
  179.0 41.7 %all-gather.11.cloned.1.call-done = bf16[3072,768]{1,0:T(8,128)(2,1)} async-done(((bf16[192,768]{1,0:T(8,128)(2,1)}), bf16[3072,768]{1,0:T(8,128)(2,1)}) %all-gather.11.cloned.1.call-update) | async-done | bytes 4718608 | tf_op jit(solution)/shard_map/all_gather | solution.py:126
  220.7 9.5 %convert_reduce_fusion = (f32[3072]{0:T(1024)S(1)}, bf16[512,3072]{1,0:T(8,128)(2,1)S(1)}, bf16[512,3072]{1,0:T(8,128)(2,1)}) fusion(f32[512,3072]{1,0:T(8,128)} %fusion.39, f32[3072]{0:T(1024)S(1)} %convert_element_type.199, bf16[512,768]{1,0:T(8,128)(2,1)} %fusion.20, bf16[3072,768]{1,0:T(8,128)(2,1)} %all-gather.11.cloned.1.call-done), kind=kOutput, calls=%fused_computation.10 | convolution fusion | flops 2444227584 | bytes 18112512 | tf_op jit(solution)/shard_map/td,fd->tf/dot_general | solution.py:32
  230.2 3.0 multiply_reduce_fusion.1
  233.2 2.0 fusion.42
  236.5 2.2 fusion.46
  238.8 3.2 convolution_convert_fusion
  242.0 2.3 copy.64
  244.6 13.7 %multiply_reduce_fusion = (f32[12,512]{1,0:T(8,128)S(1)}, f32[12,512,512]{1,2,0:T(8,128)}) fusion(f32[12,512]{1,0:T(8,128)S(1)} %log_add_fusion, f32[12,512,512]{1,2,0:T(8,128)} %copy-done, pred[512,512]{0,1:T(8,128)(4,1)S(1)} %broadcast_compare_fusion, bf16[512,12,64]{0,2,1:T(8,128)(2,1)} %bitcast.111, bf16[512,12,64]{0,2,1:T(8,128)(2,1)} %bitcast.109), kind=kOutput, calls=%fused_computation.2 | convolution fusion | flops 418375680 | bytes 27049984 | tf_op jit(solution)/shard_map/while/body/eval_jaxpr/qhe,khe->hqk/dot_general | solution.py:32
  258.4 7.2 %multiply_convert_fusion = bf16[12,512,512]{1,2,0:T(8,128)(2,1)S(1)} fusion(f32[12,512,512]{1,2,0:T(8,128)} %get-tuple-element.117, f32[12,512]{1,0:T(8,128)S(1)} %get-tuple-element.116, f32[12,512]{1,0:T(8,128)S(1)} %log_add_fusion, f32[12,512,512]{1,2,0:T(8,128)S(1)} %bitcast.104, pred[512,512]{0,1:T(8,128)(4,1)S(1)} %broadcast_compare_fusion), kind=kLoop, calls=%fused_computation.1 | loop fusion | flops 18874368 | bytes 31768576 | tf_op jit(solution)/shard_map/while/body/eval_jaxpr/convert_element_type | solution.py:198
  265.6 2.9 multiply_convert_fusion.3
  268.5 1.2 convert_reduce_fusion.5
  269.7 3.4 convert_reduce_fusion.4
  274.0 4.9 fusion.25
  279.3 8.4 %fusion.47 = f32[3072,768]{1,0:T(8,128)} fusion(bf16[512,3072]{1,0:T(8,128)(2,1)} %get-tuple-element.106, bf16[512,768]{1,0:T(8,128)(2,1)} %fusion.20), kind=kOutput, calls=%fused_computation.94 | convolution fusion | flops 2415919104 | bytes 13369344 | tf_op jit(solution)/shard_map/tf,td->fd/dot_general | solution.py:32
  288.4 8.9 %fusion.38 = f32[768,3072]{1,0:T(8,128)} fusion(bf16[512,3072]{1,0:T(8,128)(2,1)} %copy-done.32, f32[512,768]{1,0:T(8,128)} %copy-done.5, f32[768]{0:T(1024)S(1)} %copy-done.16, f32[768]{0:T(1024)S(1)} %convert_element_type.196, f32[512]{0:T(512)S(1)} %fusion.28, f32[512]{0:T(512)S(1)} %broadcast_multiply_fusion.1), kind=kOutput, calls=%fused_computation.86 | convolution fusion | flops 2417885184 | bytes 14166016 | tf_op jit(solution)/shard_map/td,tf->df/dot_general | solution.py:32
  298.0 7.2 %multiply_convert_fusion.5 = bf16[512,768]{1,0:T(8,128)(2,1)} fusion(f32[512,768]{1,0:T(8,128)} %copy-done.5, bf16[512,3072]{1,0:T(8,128)(2,1)} %get-tuple-element.106, bf16[3072,768]{1,0:T(8,128)(2,1)} %all-gather.11.cloned.1.call-done, f32[768]{0:T(1024)S(1)} %convert_element_type.201, f32[512]{0:T(512)S(1)} %compare_convert_fusion), kind=kOutput, calls=%fused_computation.52 | convolution fusion | flops 2417491968 | bytes 10228736 | tf_op jit(solution)/shard_map/dot_general | solution.py:137
  305.2 4.3 all-to-all-start.1
  309.5 5.0 fusion.40
  314.6 1.1 copy-done.6
  318.5 80.6 %reduce-scatter.15.cloned.1.call-done = f32[48,2304]{1,0:T(8,128)} async-done(((f32[768,2304]{1,0:T(8,128)}), f32[48,2304]{1,0:T(8,128)}) %reduce-scatter.15.cloned.1.call-update) | async-done | bytes 442384 | tf_op jit(solution)/shard_map/reduce_scatter | solution.py:221
  401.2 2.8 add_convert_fusion.1
  404.0 4.3 all-to-all-start.3
  408.4 105.7 %reduce-scatter.23.cloned.1.call-done = f32[192,768]{1,0:T(8,128)} async-done(((f32[3072,768]{1,0:T(8,128)}), f32[192,768]{1,0:T(8,128)}) %reduce-scatter.23.cloned.1.call-update) | async-done | bytes 589840 | tf_op jit(solution)/shard_map/reduce_scatter | solution.py:165
  516.1 112.9 %reduce-scatter.19.cloned.1.call-done = f32[48,3072]{1,0:T(8,128)} async-done(((f32[768,3072]{1,0:T(8,128)}), f32[48,3072]{1,0:T(8,128)}) %reduce-scatter.19.cloned.1.call-update) | async-done | bytes 589840 | tf_op jit(solution)/shard_map/reduce_scatter | solution.py:164
  629.0 1.8 convert_element_type.227
  632.6 60.3 %all-reduce.18 = (f32[768]{0:T(1024)S(1)}, f32[768]{0:T(1024)S(1)}, f32[768]{0:T(1024)S(1)}, f32[768]{0:T(1024)S(1)}, f32[768]{0:T(1024)S(1)}, /*index=5*/f32[76...) all-reduce(f32[768]{0:T(1024)S(1)} %get-tuple-element.68, ...), channel_id=2, replica_groups=mesh['dp'=16,'fsdp'=2] {'dp'}, use_global_device_ids=true, to_apply=%region_15.16.clone | all-reduce | flops 9216 | bytes 73728
  693.5 5.5 all-reduce.19
  704.3 1.6 convert_element_type.228
  706.0 2.1 copy.89
  (186 shorter events, 26.2 us)
Async XLA Ops:
  7.2 27.0 %copy-start.15 = (bf16[192,384]{1,0:T(8,128)(2,1)S(1)}, bf16[192,384]{1,0:T(8,128)(2,1)}, u32[]{:S(2)}) copy-start(bf16[192,384]{1,0:T(8,128)(2,1)} %param.32) | copy-start | bytes 442372
  7.2 34.0 %copy-start.21 = (s32[1,4]{1,0:T(1,128)S(1)}, s32[1,4]{1,0:T(1,128)}, u32[]{:S(2)}) copy-start(s32[1,4]{1,0:T(1,128)} %param.19) | copy-start | bytes 52
  7.2 139.5 %all-gather.5.cloned.1.call-start = ((), (), s32[]{:S(2)}) async-start(), calls=%async_computation.12 | async-start | bytes 3760128 | tf_op jit(solution)/shard_map/all_gather | solution.py:74
  15.9 153.0 %all-gather.7.cloned.1.call-start = ((), (), s32[]{:S(2)}) async-start(), calls=%async_computation.13 | async-start | bytes 1253376 | tf_op jit(solution)/shard_map/all_gather | solution.py:77
  20.9 49.6 %copy-start.18 = (u32[32]{0:T(128)S(1)}, u32[32]{0:T(128)}, u32[]{:S(2)}) copy-start(u32[32]{0:T(128)} %constant.73) | copy-start | bytes 388
  20.9 51.5 %copy-start.22 = (bf16[48]{0:T(256)(128)(2,1)S(1)}, bf16[48]{0:T(256)(128)(2,1)}, u32[]{:S(2)}) copy-start(bf16[48]{0:T(256)(128)(2,1)} %param.28) | copy-start | bytes 292
  21.0 51.7 %copy-start.23 = (bf16[48]{0:T(256)(128)(2,1)S(1)}, bf16[48]{0:T(256)(128)(2,1)}, u32[]{:S(2)}) copy-start(bf16[48]{0:T(256)(128)(2,1)} %param.29) | copy-start | bytes 292
  21.0 51.9 %copy-start.24 = (bf16[48]{0:T(256)(128)(2,1)S(1)}, bf16[48]{0:T(256)(128)(2,1)}, u32[]{:S(2)}) copy-start(bf16[48]{0:T(256)(128)(2,1)} %param.27) | copy-start | bytes 292
  21.0 52.2 %copy-start.25 = (bf16[48]{0:T(256)(128)(2,1)S(1)}, bf16[48]{0:T(256)(128)(2,1)}, u32[]{:S(2)}) copy-start(bf16[48]{0:T(256)(128)(2,1)} %param.24) | copy-start | bytes 292
  21.0 52.4 %copy-start.26 = (bf16[48]{0:T(256)(128)(2,1)S(1)}, bf16[48]{0:T(256)(128)(2,1)}, u32[]{:S(2)}) copy-start(bf16[48]{0:T(256)(128)(2,1)} %param.25) | copy-start | bytes 292
  21.0 52.6 %copy-start.27 = (bf16[48]{0:T(256)(128)(2,1)S(1)}, bf16[48]{0:T(256)(128)(2,1)}, u32[]{:S(2)}) copy-start(bf16[48]{0:T(256)(128)(2,1)} %param.21) | copy-start | bytes 292
  21.0 52.8 %copy-start.28 = (bf16[48]{0:T(256)(128)(2,1)S(1)}, bf16[48]{0:T(256)(128)(2,1)}, u32[]{:S(2)}) copy-start(bf16[48]{0:T(256)(128)(2,1)} %param.22) | copy-start | bytes 292
  21.0 53.0 %copy-start.29 = (bf16[48]{0:T(256)(128)(2,1)S(1)}, bf16[48]{0:T(256)(128)(2,1)}, u32[]{:S(2)}) copy-start(bf16[48]{0:T(256)(128)(2,1)} %param.33) | copy-start | bytes 292
  21.0 53.3 %copy-start.30 = (bf16[192]{0:T(256)(128)(2,1)S(1)}, bf16[192]{0:T(256)(128)(2,1)}, u32[]{:S(2)}) copy-start(bf16[192]{0:T(256)(128)(2,1)} %param.31) | copy-start | bytes 1156
  21.1 120.3 %copy-start.19 = (s32[512]{0:T(512)S(1)}, s32[512]{0:T(512)}, u32[]{:S(2)}) copy-start(s32[512]{0:T(512)} %param.20) | copy-start | bytes 6148
  21.1 150.7 %all-gather.9.cloned.1.call-start = ((), (), s32[]{:S(2)}) async-start(), calls=%async_computation.14 | async-start | bytes 5013504 | tf_op jit(solution)/shard_map/all_gather | solution.py:124
  28.2 27.9 %all-to-all-start = ((bf16[16,32,768]{2,1,0:T(8,128)(2,1)}), bf16[16,32,768]{2,1,0:T(8,128)(2,1)S(1)}, u32[]{:S(2)}, u32[]{:S(2)}) async-start(bf16[16,32,768]{2,1,0:T(8,128)(2,1)} %bitcast.119), calls=%async_computation | async-start | bytes 1572864 | tf_op jit(solution)/shard_map/all_to_all | solution.py:59
  34.1 186.5 %all-gather.11.cloned.1.call-start = ((), (), s32[]{:S(2)}) async-start(), calls=%async_computation.15 | async-start | bytes 5013504 | tf_op jit(solution)/shard_map/all_gather | solution.py:126
  56.1 89.2 %all-to-all-start.2 = ((bf16[16,32,768]{2,1,0:T(8,128)(2,1)}), bf16[16,32,768]{2,1,0:T(8,128)(2,1)S(1)}, u32[]{:S(2)}, u32[]{:S(2)}) async-start(bf16[16,32,768]{2,1,0:T(8,128)(2,1)} %bitcast.13), calls=%async_computation.2 | async-start | bytes 1572864 | tf_op jit(solution)/shard_map/all_to_all | solution.py:60
  70.4 246.2 %reduce-scatter.17.cloned.1.call-start = ((), (), s32[]{:S(2)}) async-start(), calls=%async_computation.17 | async-start | bytes 2506752 | tf_op jit(solution)/shard_map/reduce_scatter | solution.py:222
  146.7 4.4 copy-start.11
  153.4 6.4 copy-start.3
  155.2 4.7 copy-start.1
  159.8 4.6 copy-start
  159.9 4.6 copy-start.7
  171.4 58.8 %copy-start.5 = (f32[512,768]{1,0:T(8,128)}, f32[512,768]{1,0:T(8,128)S(1)}, u32[]{:S(2)}) copy-start(f32[512,768]{1,0:T(8,128)S(1)} %get-tuple-element.114) | copy-start | bytes 4718596
  220.7 9.5 %copy-start.20 = (bf16[768,3072]{1,0:T(8,128)(2,1)S(1)}, bf16[768,3072]{1,0:T(8,128)(2,1)}, u32[]{:S(2)}) copy-start(bf16[768,3072]{1,0:T(8,128)(2,1)} %all-gather.9.cloned.1.call-done) | copy-start | bytes 14155780
  230.2 3.0 copy-start.32
  235.2 1.3 copy-start.13
  244.3 154.8 %reduce-scatter.15.cloned.1.call-start = ((), (), s32[]{:S(2)}) async-start(), calls=%async_computation.16 | async-start | bytes 7520256 | tf_op jit(solution)/shard_map/reduce_scatter | solution.py:221
  244.6 13.8 %slice-start = ((s8[12582912]{0:T(1024)(128)(4,1)}), s8[4194304]{0:T(1024)(128)(4,1)S(1)}, s32[]{:S(2)}) async-start(s8[12582912]{0:T(1024)(128)(4,1)} %bitcast.103), calls=%async_computation.24 | async-start | bytes 8388608
  244.6 13.8 %slice-start.1 = ((s8[12582912]{0:T(1024)(128)(4,1)}), s8[4194304]{0:T(1024)(128)(4,1)S(1)}, s32[]{:S(2)}) async-start(s8[12582912]{0:T(1024)(128)(4,1)} %bitcast.103), calls=%async_computation.25 | async-start | bytes 8388608
  244.6 13.8 %slice-start.2 = ((s8[12582912]{0:T(1024)(128)(4,1)}), s8[4194304]{0:T(1024)(128)(4,1)S(1)}, s32[]{:S(2)}) async-start(s8[12582912]{0:T(1024)(128)(4,1)} %bitcast.103), calls=%async_computation.26 | async-start | bytes 8388608
  258.4 7.2 %copy-start.4 = (bf16[512,768]{0,1:T(8,128)(2,1)S(1)}, bf16[512,768]{0,1:T(8,128)(2,1)}, u32[]{:S(2)}) copy-start(bf16[512,768]{0,1:T(8,128)(2,1)} %copy-done.3) | copy-start | bytes 2359300
  265.6 2.9 copy-start.2
  268.5 1.2 copy-start.8
  269.7 3.4 copy-start.10
  269.7 4.3 copy-start.12
  269.7 4.3 copy-start.14
  279.0 235.1 %reduce-scatter.23.cloned.1.call-start = ((), (), s32[]{:S(2)}) async-start(), calls=%async_computation.20 | async-start | bytes 10027008 | tf_op jit(solution)/shard_map/reduce_scatter | solution.py:165
  287.7 341.3 %reduce-scatter.19.cloned.1.call-start = ((), (), s32[]{:S(2)}) async-start(), calls=%async_computation.18 | async-start | bytes 10027008 | tf_op jit(solution)/shard_map/reduce_scatter | solution.py:164
  305.2 98.8 %all-to-all-start.1 = ((bf16[16,32,768]{2,1,0:T(8,128)(2,1)}), bf16[16,32,768]{2,1,0:T(8,128)(2,1)}, u32[]{:S(2)}, u32[]{:S(2)}) async-start(bf16[16,32,768]{2,1,0:T(8,128)(2,1)} %bitcast.120), calls=%async_computation.1 | async-start | bytes 1572864 | tf_op jit(solution)/shard_map/all_to_all | solution.py:258
  309.5 389.6 %reduce-scatter.27.cloned.1.call-start = ((), (), s32[]{:S(2)}) async-start(), calls=%async_computation.22 | async-start | bytes 294912
  314.6 1.2 copy-start.6
  318.4 382.3 %reduce-scatter.25.cloned.1.call-start = ((), (), s32[]{:S(2)}) async-start(), calls=%async_computation.21 | async-start | bytes 884736
  404.0 295.1 %all-to-all-start.3 = ((bf16[16,32,768]{2,1,0:T(8,128)(2,1)}), bf16[16,32,768]{2,1,0:T(8,128)(2,1)S(1)}, u32[]{:S(2)}, u32[]{:S(2)}) async-start(bf16[16,32,768]{2,1,0:T(8,128)(2,1)} %bitcast.114), calls=%async_computation.3 | async-start | bytes 1572864 | tf_op jit(solution)/shard_map/all_to_all | solution.py:261
  408.3 294.2 %reduce-scatter.29.cloned.1.call-start = ((), (), s32[]{:S(2)}) async-start(), calls=%async_computation.23 | async-start | bytes 589824
  516.1 188.3 %reduce-scatter.21.cloned.1.call-start = ((), (), s32[]{:S(2)}) async-start(), calls=%async_computation.19 | async-start | bytes 442368 | tf_op jit(solution)/shard_map/reduce_scatter | solution.py:236
  (4 other events, 3.2 us)
Sparse Core Ops, SparseCore 0:
  16.0 54.1 all-gather.4
  72.6 39.9 all-gather.6
  114.8 51.9 all-gather.8
  169.0 51.6 all-gather.10
  244.4 61.7 reduce-scatter.16
  310.1 88.9 reduce-scatter.14
  403.2 110.8 reduce-scatter.22
  518.1 110.8 reduce-scatter.18
  631.8 10.6 reduce-scatter.26
  644.7 15.3 reduce-scatter.24
  662.9 13.1 reduce-scatter.28
  678.8 12.0 reduce-scatter.20
where the time goes:
time: 722 us; the launch traced here: 716 us
  waiting for transfers between devices  356 us (49%)
  blocking collectives  160 us (22%)
  matrix products  94.2 us (13%)
  starting transfers between devices  29.8 us (4%)
  local copies, waits for them, and re-layouts  29.7 us (4%)
  other arithmetic  29.2 us (4%)
  between operations  17.9 us (2%)
    unnamed x2, blocking collectives  126 us
    reduce_scatter x1, waiting for transfers between devices, local(): lax.psum_scatter(grad_up, 'dp', scatter_dimension=0, tiled=True)  113 us
    reduce_scatter x1, waiting for transfers between devices, local(): lax.psum_scatter(grad_down, 'dp', scatter_dimension=0, tiled=True)  106 us
    reduce_scatter x1, waiting for transfers between devices, local(): lax.psum_scatter(grad_project, 'dp', scatter_dimension=0, tiled=True)  80.6 us
    dot_general x14, matrix products, matmul(): jnp.einsum(pattern, left_side, right_side, preferred_element_type=jnp.flo...  72.9 us
    all_gather x1, waiting for transfers between devices, local(): lax.all_gather(down_part, 'dp', axis=0, tiled=True)  41.7 us
    unnamed x108, local copies, waits for them, and re-layouts  18.6 us
    all_to_all x1, waiting for transfers between devices, local(): lax.all_to_all(patches, 'dp', split_axis=0, concat_axis=0, tiled=True)  14.7 us
  transfers between devices with their start and end apart: 16, of which 5 were waited for; matrix products, arithmetic and copies ran while one was open for 17% of the time, Pallas kernels for 0%

commit v1 on v0

--- a/solution.py
+++ b/solution.py
@@ -8,6 +8,18 @@
 NORM_EPSILON = 1e-12
 MASK_VALUE = -1e30
 ROOT_HALF = 0.7071067811865476
+
+
+def gather_by_bits(x, axis, dim):
+    ways, here = (lax.axis_size(axis), lax.axis_index(axis))
+    grown, reach = (x, 1)
+    while reach < ways:
+        theirs = lax.ppermute(grown, axis, [(d, d ^ reach) for d in range(ways)])
+        mine_first = jnp.concatenate([grown, theirs], axis=dim)
+        theirs_first = jnp.concatenate([theirs, grown], axis=dim)
+        grown = jnp.where(here & reach == 0, mine_first, theirs_first)
+        reach = 2 * reach
+    return grown
 
 
 def norm_rows(values, norm_gain, norm_shift):
@@ -123,7 +135,7 @@
         lax.all_gather(second_shift, "dp", axis=0, tiled=True),
         lax.all_gather(up_part, "dp", axis=0, tiled=True),
         lax.all_gather(up_bias, "dp", axis=0, tiled=True),
-        lax.all_gather(down_part, "dp", axis=0, tiled=True),
+        gather_by_bits(down_part, "dp", 0),
         lax.all_gather(down_bias, "dp", axis=0, tiled=True),
     )
     gain_two = mlp_set[0].astype(jnp.float32)

time: 722 us -> 822 us (1.14)
  waiting for transfers between devices: 356 us -> 446 us
    ppermute x0 -> x4, waiting for transfers between devices: none -> 86.6 us  [gather_by_bits(): theirs = lax.ppermute(grown, axis, [(d, d ^ reach) for d in range(ways)])]
    reduce_scatter x1, waiting for transfers between devices: 80.6 us -> 89.9 us  [local(): lax.psum_scatter(grad_project, 'dp', scatter_dimension=0, tiled=True)]
    select_n x0 -> x3, other arithmetic: none -> 8.96 us  [gather_by_bits(): grown = jnp.where(here & reach == 0, mine_first, theirs_first)]
    unnamed x108 -> x118, local copies, waits for them, and re-layouts: 18.6 us -> 16.7 us
  transfers between devices with their start and end apart: 16 -> 20, of which waited for: 5 -> 9; matrix products, arithmetic and copies ran while one was open for 17% -> 16% of each run, Pallas kernels for 0% -> 0%
where the time goes in v1:
time: 822 us; the launch traced here: 817 us
  waiting for transfers between devices  446 us (54%)
  blocking collectives  159 us (19%)
  matrix products  94.6 us (12%)
  other arithmetic  37.1 us (5%)
  starting transfers between devices  33.8 us (4%)
  local copies, waits for them, and re-layouts  27.9 us (3%)
  between operations  17.7 us (2%)
    unnamed x2, blocking collectives  126 us
    reduce_scatter x1, waiting for transfers between devices, local(): lax.psum_scatter(grad_up, 'dp', scatter_dimension=0, tiled=True)  113 us
    reduce_scatter x1, waiting for transfers between devices, local(): lax.psum_scatter(grad_down, 'dp', scatter_dimension=0, tiled=True)  100 us
    reduce_scatter x1, waiting for transfers between devices, local(): lax.psum_scatter(grad_project, 'dp', scatter_dimension=0, tiled=True)  89.9 us
    ppermute x4, waiting for transfers between devices, gather_by_bits(): theirs = lax.ppermute(grown, axis, [(d, d ^ reach) for d in range(ways)])  86.6 us
    dot_general x14, matrix products, matmul(): jnp.einsum(pattern, left_side, right_side, preferred_element_type=jnp.flo...  72.7 us
    all_gather x1, waiting for transfers between devices, local(): lax.all_gather(down_part, 'dp', axis=0, tiled=True)  41.4 us
    unnamed x118, local copies, waits for them, and re-layouts  16.7 us
  transfers between devices with their start and end apart: 20, of which 9 were waited for; matrix products, arithmetic and copies ran while one was open for 16% of the time, Pallas kernels for 0%

profile of v1, /device:TPU:0, one launch (start us, length us, event | category | flops | bytes accessed | tf_op | source)
XLA Modules:
  0.0 816.5 jit_solution(17445156893522034238)
XLA Ops:
  7.2 8.7 %all_gather.58 = bf16[48,2304]{1,0:T(8,128)(2,1)} all-gather(bf16[48,1152]{1,0:T(8,128)(2,1)} %param.23), channel_id=1, replica_groups=mesh['dp'=16,'fsdp'=2] {'fsdp'}, dimensions={1}, use_global_device_ids=true | all-gather | bytes 331776 | tf_op jit(solution)/shard_map/all_gather | solution.py:78
  16.0 4.9 all_gather.62
  21.1 7.0 all_gather.67
  28.2 6.0 all-to-all-start
  34.2 6.9 all_gather.70
  41.3 14.7 %all-to-all-done = bf16[16,32,768]{2,1,0:T(8,128)(2,1)S(1)} async-done(((bf16[16,32,768]{2,1,0:T(8,128)(2,1)}), bf16[16,32,768]{2,1,0:T(8,128)(2,1)S(1)}, u32[]{:S(2)}, u32[]{:S(2)}) %all-to-all-start) | async-done | bytes 786464 | tf_op jit(solution)/shard_map/all_to_all | solution.py:71
  56.1 14.5 %all-to-all-start.2 = ((bf16[16,32,768]{2,1,0:T(8,128)(2,1)}), bf16[16,32,768]{2,1,0:T(8,128)(2,1)S(1)}, u32[]{:S(2)}, u32[]{:S(2)}) async-start(bf16[16,32,768]{2,1,0:T(8,128)(2,1)} %bitcast.13), calls=%async_computation.2 | async-start | bytes 1572864 | tf_op jit(solution)/shard_map/all_to_all | solution.py:72
  74.8 66.1 %all-reduce.20 = (bf16[768]{0:T(1024)(128)(2,1)S(1)}, bf16[768]{0:T(1024)(128)(2,1)S(1)}, bf16[768]{0:T(1024)(128)(2,1)S(1)}, bf16[768]{0:T(1024)(128)(2,1)S(1)}...) all-reduce(bf16[768]{0:T(1024)(128)(2,1)S(1)} %dynamic-update-slice, ...), channel_id=1, replica_groups=mesh['dp'=16,'fsdp'=2] {'dp'}, use_global_device_ids=true, to_apply=%add.1 | all-reduce | flops 9216 | bytes 36864
  141.5 3.0 scatter_custom_fusion
  147.0 4.3 fusion.53
  153.7 1.7 copy.62
  155.4 2.6 copy.60
  158.0 2.1 fusion.13
  160.1 2.6 fusion
  162.7 2.1 copy-done
  164.7 4.5 fusion.31
  169.3 2.4 fusion.52
  172.1 7.2 fusion.47
  179.3 41.4 %all-gather.11.cloned.1.call-done = bf16[3072,768]{1,0:T(8,128)(2,1)} async-done(((bf16[192,768]{1,0:T(8,128)(2,1)}), bf16[3072,768]{1,0:T(8,128)(2,1)}) %all-gather.11.cloned.1.call-update) | async-done | bytes 4718608 | tf_op jit(solution)/shard_map/all_gather | solution.py:160
  220.7 9.5 %convert_reduce_fusion = (f32[3072]{0:T(1024)S(1)}, bf16[512,3072]{1,0:T(8,128)(2,1)S(1)}, bf16[512,3072]{1,0:T(8,128)(2,1)}) fusion(f32[512,3072]{1,0:T(8,128)} %fusion.47, f32[3072]{0:T(1024)S(1)} %convert_element_type.199, bf16[512,768]{1,0:T(8,128)(2,1)} %fusion.27, bf16[3072,768]{1,0:T(8,128)(2,1)} %all-gather.11.cloned.1.call-done), kind=kOutput, calls=%fused_computation.10 | convolution fusion | flops 2444227584 | bytes 18112512 | tf_op jit(solution)/shard_map/td,fd->tf/dot_general | solution.py:44
  230.2 3.5 multiply_reduce_fusion.1
  233.7 2.0 fusion.50
  237.1 2.2 fusion.54
  239.3 3.2 convolution_convert_fusion
  242.5 2.3 copy.64
  245.1 13.7 %multiply_reduce_fusion = (f32[12,512]{1,0:T(8,128)S(1)}, f32[12,512,512]{1,2,0:T(8,128)}) fusion(f32[12,512]{1,0:T(8,128)S(1)} %log_add_fusion, f32[12,512,512]{1,2,0:T(8,128)} %copy-done, pred[512,512]{0,1:T(8,128)(4,1)S(1)} %broadcast_compare_fusion, bf16[512,12,64]{0,2,1:T(8,128)(2,1)} %bitcast.109, bf16[512,12,64]{0,2,1:T(8,128)(2,1)} %bitcast.107), kind=kOutput, calls=%fused_computation.2 | convolution fusion | flops 418375680 | bytes 27049984 | tf_op jit(solution)/shard_map/while/body/eval_jaxpr/qhe,khe->hqk/dot_general | solution.py:44
  258.9 7.2 multiply_convert_fusion
  267.4 2.9 multiply_convert_fusion.3
  270.3 3.4 convert_reduce_fusion.4
  274.5 5.0 fusion.32
  280.0 8.4 %fusion.55 = f32[3072,768]{1,0:T(8,128)} fusion(bf16[512,3072]{1,0:T(8,128)(2,1)} %get-tuple-element.106, bf16[512,768]{1,0:T(8,128)(2,1)} %fusion.27), kind=kOutput, calls=%fused_computation.106 | convolution fusion | flops 2415919104 | bytes 13369344 | tf_op jit(solution)/shard_map/tf,td->fd/dot_general | solution.py:44
  289.1 8.9 %fusion.46 = f32[768,3072]{1,0:T(8,128)} fusion(bf16[512,3072]{1,0:T(8,128)(2,1)} %copy-done.37, f32[512,768]{1,0:T(8,128)} %copy-done.5, f32[768]{0:T(1024)S(1)} %copy-done.19, f32[768]{0:T(1024)S(1)} %convert_element_type.196, f32[512]{0:T(512)S(1)} %fusion.35, f32[512]{0:T(512)S(1)} %broadcast_multiply_fusion.1), kind=kOutput, calls=%fused_computation.98 | convolution fusion | flops 2417885184 | bytes 14166016 | tf_op jit(solution)/shard_map/td,tf->df/dot_general | solution.py:44
  300.6 2.1 maximum_select_fusion.6
  303.3 15.3 %collective-permute-done.1 = bf16[384,768]{1,0:T(8,128)(2,1)} collective-permute-done((bf16[384,768]{1,0:T(8,128)(2,1)}, bf16[384,768]{1,0:T(8,128)(2,1)}, u32[]{:S(2)}, u32[]{:S(2)}) %collective-permute-start.1) | collective-permute-done | bytes 589856 | tf_op jit(solution)/shard_map/ppermute | solution.py:17
  318.6 3.1 maximum_select_fusion.5
  323.2 42.5 %collective-permute-done.2 = bf16[768,768]{1,0:T(8,128)(2,1)} collective-permute-done((bf16[768,768]{1,0:T(8,128)(2,1)}, bf16[768,768]{1,0:T(8,128)(2,1)}, u32[]{:S(2)}, u32[]{:S(2)}) %collective-permute-start.2) | collective-permute-done | bytes 1179680 | tf_op jit(solution)/shard_map/ppermute | solution.py:17
  365.7 3.8 maximum_select_fusion.2
  369.5 4.3 fusion.48
  376.4 4.4 all-to-all-start.3
  382.9 89.9 %reduce-scatter.15.cloned.1.call-done = f32[48,2304]{1,0:T(8,128)} async-done(((f32[768,2304]{1,0:T(8,128)}), f32[48,2304]{1,0:T(8,128)}) %reduce-scatter.15.cloned.1.call-update) | async-done | bytes 442384 | tf_op jit(solution)/shard_map/reduce_scatter | solution.py:233
  474.9 27.4 %collective-permute-done.3 = bf16[1536,768]{1,0:T(8,128)(2,1)} collective-permute-done((bf16[1536,768]{1,0:T(8,128)(2,1)}, bf16[1536,768]{1,0:T(8,128)(2,1)}, u32[]{:S(2)}, u32[]{:S(2)}) %collective-permute-start.3) | collective-permute-done | bytes 2359328 | tf_op jit(solution)/shard_map/ppermute | solution.py:17
  502.3 7.9 multiply_convert_fusion.5
  510.2 5.3 all-to-all-start.1
  515.6 100.2 %reduce-scatter.23.cloned.1.call-done = f32[192,768]{1,0:T(8,128)} async-done(((f32[3072,768]{1,0:T(8,128)}), f32[192,768]{1,0:T(8,128)}) %reduce-scatter.23.cloned.1.call-update) | async-done | bytes 589840 | tf_op jit(solution)/shard_map/reduce_scatter | solution.py:177
  617.8 112.9 %reduce-scatter.19.cloned.1.call-done = f32[48,3072]{1,0:T(8,128)} async-done(((f32[768,3072]{1,0:T(8,128)}), f32[48,3072]{1,0:T(8,128)}) %reduce-scatter.19.cloned.1.call-update) | async-done | bytes 589840 | tf_op jit(solution)/shard_map/reduce_scatter | solution.py:176
  730.7 1.8 convert_element_type.227
  734.3 60.3 %all-reduce.18 = (f32[768]{0:T(1024)S(1)}, f32[768]{0:T(1024)S(1)}, f32[768]{0:T(1024)S(1)}, f32[768]{0:T(1024)S(1)}, f32[768]{0:T(1024)S(1)}, /*index=5*/f32[76...) all-reduce(f32[768]{0:T(1024)S(1)} %get-tuple-element.68, ...), channel_id=2, replica_groups=mesh['dp'=16,'fsdp'=2] {'dp'}, use_global_device_ids=true, to_apply=%region_15.16.clone | all-reduce | flops 9216 | bytes 73728
  795.3 5.5 all-reduce.19
  (207 shorter events, 37.2 us)
Async XLA Ops:
  7.2 27.0 %copy-start.18 = (bf16[192,384]{1,0:T(8,128)(2,1)S(1)}, bf16[192,384]{1,0:T(8,128)(2,1)}, u32[]{:S(2)}) copy-start(bf16[192,384]{1,0:T(8,128)(2,1)} %param.32) | copy-start | bytes 442372
  7.2 34.0 %copy-start.25 = (s32[1,4]{1,0:T(1,128)S(1)}, s32[1,4]{1,0:T(1,128)}, u32[]{:S(2)}) copy-start(s32[1,4]{1,0:T(1,128)} %param.19) | copy-start | bytes 52
  7.2 139.8 %all-gather.5.cloned.1.call-start = ((), (), s32[]{:S(2)}) async-start(), calls=%async_computation.12 | async-start | bytes 3760128 | tf_op jit(solution)/shard_map/all_gather | solution.py:86
  15.9 153.3 %all-gather.7.cloned.1.call-start = ((), (), s32[]{:S(2)}) async-start(), calls=%async_computation.13 | async-start | bytes 1253376 | tf_op jit(solution)/shard_map/all_gather | solution.py:89
  20.9 49.8 %copy-start.22 = (u32[32]{0:T(128)S(1)}, u32[32]{0:T(128)}, u32[]{:S(2)}) copy-start(u32[32]{0:T(128)} %constant.86) | copy-start | bytes 388
  20.9 51.7 %copy-start.26 = (bf16[48]{0:T(256)(128)(2,1)S(1)}, bf16[48]{0:T(256)(128)(2,1)}, u32[]{:S(2)}) copy-start(bf16[48]{0:T(256)(128)(2,1)} %param.21) | copy-start | bytes 292
  21.0 51.9 %copy-start.27 = (bf16[48]{0:T(256)(128)(2,1)S(1)}, bf16[48]{0:T(256)(128)(2,1)}, u32[]{:S(2)}) copy-start(bf16[48]{0:T(256)(128)(2,1)} %param.22) | copy-start | bytes 292
  21.0 52.1 %copy-start.28 = (bf16[48]{0:T(256)(128)(2,1)S(1)}, bf16[48]{0:T(256)(128)(2,1)}, u32[]{:S(2)}) copy-start(bf16[48]{0:T(256)(128)(2,1)} %param.25) | copy-start | bytes 292
  21.0 52.3 %copy-start.29 = (bf16[48]{0:T(256)(128)(2,1)S(1)}, bf16[48]{0:T(256)(128)(2,1)}, u32[]{:S(2)}) copy-start(bf16[48]{0:T(256)(128)(2,1)} %param.24) | copy-start | bytes 292
  21.0 52.6 %copy-start.30 = (bf16[48]{0:T(256)(128)(2,1)S(1)}, bf16[48]{0:T(256)(128)(2,1)}, u32[]{:S(2)}) copy-start(bf16[48]{0:T(256)(128)(2,1)} %param.27) | copy-start | bytes 292
  21.0 52.8 %copy-start.31 = (bf16[48]{0:T(256)(128)(2,1)S(1)}, bf16[48]{0:T(256)(128)(2,1)}, u32[]{:S(2)}) copy-start(bf16[48]{0:T(256)(128)(2,1)} %param.28) | copy-start | bytes 292
  21.0 53.0 %copy-start.32 = (bf16[48]{0:T(256)(128)(2,1)S(1)}, bf16[48]{0:T(256)(128)(2,1)}, u32[]{:S(2)}) copy-start(bf16[48]{0:T(256)(128)(2,1)} %param.29) | copy-start | bytes 292
  21.0 53.2 %copy-start.33 = (bf16[48]{0:T(256)(128)(2,1)S(1)}, bf16[48]{0:T(256)(128)(2,1)}, u32[]{:S(2)}) copy-start(bf16[48]{0:T(256)(128)(2,1)} %param.33) | copy-start | bytes 292
  21.0 53.5 %copy-start.34 = (bf16[192]{0:T(256)(128)(2,1)S(1)}, bf16[192]{0:T(256)(128)(2,1)}, u32[]{:S(2)}) copy-start(bf16[192]{0:T(256)(128)(2,1)} %param.31) | copy-start | bytes 1156
  21.1 120.4 %copy-start.23 = (s32[512]{0:T(512)S(1)}, s32[512]{0:T(512)}, u32[]{:S(2)}) copy-start(s32[512]{0:T(512)} %param.20) | copy-start | bytes 6148
  21.1 151.0 %all-gather.9.cloned.1.call-start = ((), (), s32[]{:S(2)}) async-start(), calls=%async_computation.14 | async-start | bytes 5013504 | tf_op jit(solution)/shard_map/all_gather | solution.py:136
  28.2 27.9 %all-to-all-start = ((bf16[16,32,768]{2,1,0:T(8,128)(2,1)}), bf16[16,32,768]{2,1,0:T(8,128)(2,1)S(1)}, u32[]{:S(2)}, u32[]{:S(2)}) async-start(bf16[16,32,768]{2,1,0:T(8,128)(2,1)} %bitcast.118), calls=%async_computation | async-start | bytes 1572864 | tf_op jit(solution)/shard_map/all_to_all | solution.py:71
  34.1 186.6 %all-gather.11.cloned.1.call-start = ((), (), s32[]{:S(2)}) async-start(), calls=%async_computation.15 | async-start | bytes 5013504 | tf_op jit(solution)/shard_map/all_gather | solution.py:160
  56.1 89.4 %all-to-all-start.2 = ((bf16[16,32,768]{2,1,0:T(8,128)(2,1)}), bf16[16,32,768]{2,1,0:T(8,128)(2,1)S(1)}, u32[]{:S(2)}, u32[]{:S(2)}) async-start(bf16[16,32,768]{2,1,0:T(8,128)(2,1)} %bitcast.13), calls=%async_computation.2 | async-start | bytes 1572864 | tf_op jit(solution)/shard_map/all_to_all | solution.py:72
  70.6 310.3 %reduce-scatter.17.cloned.1.call-start = ((), (), s32[]{:S(2)}) async-start(), calls=%async_computation.17 | async-start | bytes 2506752 | tf_op jit(solution)/shard_map/reduce_scatter | solution.py:234
  153.7 6.4 copy-start.3
  155.4 4.7 copy-start.1
  171.7 58.5 %copy-start.5 = (f32[512,768]{1,0:T(8,128)}, f32[512,768]{1,0:T(8,128)S(1)}, u32[]{:S(2)}) copy-start(f32[512,768]{1,0:T(8,128)S(1)} %get-tuple-element.114) | copy-start | bytes 4718596
  220.7 9.5 %copy-start.24 = (bf16[768,3072]{1,0:T(8,128)(2,1)S(1)}, bf16[768,3072]{1,0:T(8,128)(2,1)}, u32[]{:S(2)}) copy-start(bf16[768,3072]{1,0:T(8,128)(2,1)} %all-gather.9.cloned.1.call-done) | copy-start | bytes 14155780
  244.8 227.9 %reduce-scatter.15.cloned.1.call-start = ((), (), s32[]{:S(2)}) async-start(), calls=%async_computation.16 | async-start | bytes 7520256 | tf_op jit(solution)/shard_map/reduce_scatter | solution.py:233
  245.1 13.8 %slice-start = ((s8[12582912]{0:T(1024)(128)(4,1)}), s8[4194304]{0:T(1024)(128)(4,1)S(1)}, s32[]{:S(2)}) async-start(s8[12582912]{0:T(1024)(128)(4,1)} %bitcast.101), calls=%async_computation.24 | async-start | bytes 8388608
  245.1 13.8 %slice-start.1 = ((s8[12582912]{0:T(1024)(128)(4,1)}), s8[4194304]{0:T(1024)(128)(4,1)S(1)}, s32[]{:S(2)}) async-start(s8[12582912]{0:T(1024)(128)(4,1)} %bitcast.101), calls=%async_computation.25 | async-start | bytes 8388608
  245.1 13.8 %slice-start.2 = ((s8[12582912]{0:T(1024)(128)(4,1)}), s8[4194304]{0:T(1024)(128)(4,1)S(1)}, s32[]{:S(2)}) async-start(s8[12582912]{0:T(1024)(128)(4,1)} %bitcast.101), calls=%async_computation.26 | async-start | bytes 8388608
  258.9 7.2 copy-start.2
  267.3 6.3 copy-start.11
  279.5 336.2 %reduce-scatter.23.cloned.1.call-start = ((), (), s32[]{:S(2)}) async-start(), calls=%async_computation.20 | async-start | bytes 10027008 | tf_op jit(solution)/shard_map/reduce_scatter | solution.py:177
  288.4 442.3 %reduce-scatter.19.cloned.1.call-start = ((), (), s32[]{:S(2)}) async-start(), calls=%async_computation.18 | async-start | bytes 10027008 | tf_op jit(solution)/shard_map/reduce_scatter | solution.py:176
  298.9 1.7 collective-permute-start
  302.8 15.8 %collective-permute-start.1 = (bf16[384,768]{1,0:T(8,128)(2,1)}, bf16[384,768]{1,0:T(8,128)(2,1)}, u32[]{:S(2)}, u32[]{:S(2)}) collective-permute-start(bf16[384,768]{1,0:T(8,128)(2,1)} %maximum_select_fusion.6), channel_id=1, source_target_pairs={{0,4},{2,6},{4,0},{6,2},{8,12},{10,14},{12,8},{14,10},{16,20},{18,... | collective-permute-start | bytes 1769480 | tf_op jit(solution)/shard_map/ppermute | solution.py:17
  321.7 44.0 %collective-permute-start.2 = (bf16[768,768]{1,0:T(8,128)(2,1)}, bf16[768,768]{1,0:T(8,128)(2,1)}, u32[]{:S(2)}, u32[]{:S(2)}) collective-permute-start(bf16[768,768]{1,0:T(8,128)(2,1)} %maximum_select_fusion.5), channel_id=1, source_target_pairs={{0,8},{2,10},{4,12},{6,14},{8,0},{10,2},{12,4},{14,6},{16,24},{18,... | collective-permute-start | bytes 3538952 | tf_op jit(solution)/shard_map/ppermute | solution.py:17
  323.2 46.3 %copy-start.12 = (bf16[12,64,512]{2,1,0:T(8,128)(2,1)S(1)}, bf16[12,64,512]{2,1,0:T(8,128)(2,1)}, u32[]{:S(2)}) copy-start(bf16[12,64,512]{2,1,0:T(8,128)(2,1)} %copy-done.11) | copy-start | bytes 2359300
  323.2 46.3 %copy-start.17 = (bf16[12,64,512]{2,1,0:T(8,128)(2,1)S(1)}, bf16[12,64,512]{2,1,0:T(8,128)(2,1)}, u32[]{:S(2)}) copy-start(bf16[12,64,512]{2,1,0:T(8,128)(2,1)} %multiply_convert_fusion.3) | copy-start | bytes 2359300
  323.2 46.3 %copy-start.36 = (bf16[12,64,512]{2,1,0:T(8,128)(2,1)S(1)}, bf16[12,64,512]{2,1,0:T(8,128)(2,1)}, u32[]{:S(2)}) copy-start(bf16[12,64,512]{2,1,0:T(8,128)(2,1)} %copy-done.35) | copy-start | bytes 2359300
  369.5 132.8 %collective-permute-start.3 = (bf16[1536,768]{1,0:T(8,128)(2,1)}, bf16[1536,768]{1,0:T(8,128)(2,1)}, u32[]{:S(2)}, u32[]{:S(2)}) collective-permute-start(bf16[1536,768]{1,0:T(8,128)(2,1)} %maximum_select_fusion.2), channel_id=1, source_target_pairs={{0,16},{2,18},{4,20},{6,22},{8,24},{10,26},{12,28},{14,30},{16,0},... | collective-permute-start | bytes 7077896 | tf_op jit(solution)/shard_map/ppermute | solution.py:17
  374.7 8.2 %copy-start.21 = (bf16[768]{0:T(1024)(128)(2,1)S(1)}, bf16[768]{0:T(1024)(128)(2,1)}, u32[]{:S(2)}) copy-start(bf16[768]{0:T(1024)(128)(2,1)} %get-tuple-element.99) | copy-start | bytes 4612
  376.4 125.9 %copy-start.6 = (f32[512,768]{1,0:T(8,128)S(1)}, f32[512,768]{1,0:T(8,128)}, u32[]{:S(2)}) copy-start(f32[512,768]{1,0:T(8,128)} %copy-done.5) | copy-start | bytes 4718596
  376.4 133.8 %all-to-all-start.3 = ((bf16[16,32,768]{2,1,0:T(8,128)(2,1)}), bf16[16,32,768]{2,1,0:T(8,128)(2,1)S(1)}, u32[]{:S(2)}, u32[]{:S(2)}) async-start(bf16[16,32,768]{2,1,0:T(8,128)(2,1)} %bitcast.113), calls=%async_computation.3 | async-start | bytes 1572864 | tf_op jit(solution)/shard_map/all_to_all | solution.py:273
  380.8 420.0 %reduce-scatter.27.cloned.1.call-start = ((), (), s32[]{:S(2)}) async-start(), calls=%async_computation.22 | async-start | bytes 294912
  382.7 419.8 %reduce-scatter.25.cloned.1.call-start = ((), (), s32[]{:S(2)}) async-start(), calls=%async_computation.21 | async-start | bytes 884736
  510.2 290.6 %all-to-all-start.1 = ((bf16[16,32,768]{2,1,0:T(8,128)(2,1)}), bf16[16,32,768]{2,1,0:T(8,128)(2,1)S(1)}, u32[]{:S(2)}, u32[]{:S(2)}) async-start(bf16[16,32,768]{2,1,0:T(8,128)(2,1)} %bitcast.119), calls=%async_computation.1 | async-start | bytes 1572864 | tf_op jit(solution)/shard_map/all_to_all | solution.py:270
  515.5 218.8 %copy-start.20 = (f32[768]{0:T(1024)S(1)}, f32[768]{0:T(1024)}, u32[]{:S(2)}) copy-start(f32[768]{0:T(1024)} %get-tuple-element.70) | copy-start | bytes 9220
  515.5 288.8 %reduce-scatter.29.cloned.1.call-start = ((), (), s32[]{:S(2)}) async-start(), calls=%async_computation.23 | async-start | bytes 589824
  617.8 188.3 %reduce-scatter.21.cloned.1.call-start = ((), (), s32[]{:S(2)}) async-start(), calls=%async_computation.19 | async-start | bytes 442368 | tf_op jit(solution)/shard_map/reduce_scatter | solution.py:248
  (13 other events, 34.5 us)
Sparse Core Ops, SparseCore 0:
  16.1 54.1 all-gather.4
  72.6 39.9 all-gather.6
  114.9 51.9 all-gather.8
  169.0 51.6 all-gather.10
  245.0 61.9 reduce-scatter.16
  310.9 161.8 reduce-scatter.14
  476.9 138.8 reduce-scatter.22
  619.8 110.8 reduce-scatter.18
  733.5 10.6 reduce-scatter.26
  746.4 15.3 reduce-scatter.24
  764.6 13.1 reduce-scatter.28
  780.5 12.1 reduce-scatter.20
